TPU v7x, 128 devices: a whole 4x4x4 slice. The times are simulated.
128 devices in a mesh: member: 8 (over y_hi, z), lat: 16 (over y_lo, x, core).
Axes of the slice: x: 4, y: 4 (y_hi: 2, y_lo: 2; y = y_hi * 2 + y_lo), z: 4, core: 2. Of those that a mesh axis runs over, the one named last changes fastest.
Arguments:
- ensemble_state: float32 [3, 512, 128, 256], P(None, 'member', 'lat'), may hold values from -6 to 6
- obs_cell: int32 [16, 8, 256], replicated, may hold values from 0 to 255
- obs_value: float32 [16, 8, 256], replicated, may hold values from -6 to 6
- obs_prec: float32 [16, 8, 256], replicated, may hold values from 0.5 to 4
Outputs:
- analysis_a: float32 [3, 512, 128, 256], P(None, 'member', 'lat')
Inputs may be any that keep to these rules, and one draw needn't show every extreme that they name: `obs_cell`: each entry is a cell of its patch of 8 by 32 cells, counted row by row.
All inputs are finite; a program needn't handle non-finite values.
Results may differ from a plain program's by a relative error of at most 0.0003.
Values sent between devices are 32-bit elements; how exact they have to be, the bound alone decides.
A program may use at most 128 MiB of HBM per device.

v0:
```python
import math

import jax
import jax.numpy as jnp
from jax import lax
from jax.experimental import pallas as pl
from jax.experimental.pallas import tpu as pltpu
from jax.sharding import PartitionSpec as P

MESH = pl.DeviceIdType.MESH
F32 = jnp.float32
BF16 = jnp.bfloat16
NM = 8
NL = 16
ENS = 512
LOC = 64
ROWS = 8
LON = 256
CELLS = 256
DT = 0.3
NN = (((1,), (0,)), ((), ()))
NT = (((1,), (1,)), ((), ()))
BLOCKS = ((0, 0), (0, 1), (1, 1))


def dot(a, b, dims=NN):
    return lax.dot_general(a, b, dims, preferred_element_type=F32)


def split(v):
    high = v.astype(BF16)
    low = (v - high.astype(F32)).astype(BF16)
    return high, low


def iota(shape, dim):
    return lax.broadcasted_iota(jnp.int32, shape, dim)


def exchange_lanes(v, halves, evens):
    a0 = jnp.where(halves, v[0], pltpu.roll(v[2], 64, 1))
    a2 = jnp.where(halves, pltpu.roll(v[0], 64, 1), v[2])
    a1 = jnp.where(halves, v[1], pltpu.roll(v[3], 64, 1))
    a3 = jnp.where(halves, pltpu.roll(v[1], 64, 1), v[3])
    o0 = jnp.where(evens, a0, pltpu.roll(a1, 32, 1))
    o1 = jnp.where(evens, pltpu.roll(a0, 96, 1), a1)
    o2 = jnp.where(evens, a2, pltpu.roll(a3, 32, 1))
    o3 = jnp.where(evens, pltpu.roll(a2, 96, 1), a3)
    return [o0, o1, o2, o3]


def row_times(row, mat_h, mat_l, dims=NN):
    high = row.astype(BF16).astype(F32)
    lhs = jnp.concatenate([high, row - high, jnp.zeros((6, row.shape[1]), F32)], axis=0)
    lhs = lhs.astype(BF16)
    first = dot(lhs, mat_h, dims)
    second = dot(lhs, mat_l, dims)
    return first[0:1] + first[1:2] + second[0:1]


def kernel(
    xs, cell, val, prec, out,
    ht, hb, pk, rh, xf, sh, sl, g0, gs, gr, ds_, dr, co,
    yh, yl, zh, zl, mh, ml, bh, bl, qh, ql, gh, gl, mf, rf,
    xh, xl, ao, ro,
    h_send, h_recv, o_send, o_recv, f_send, f_recv, g_send, g_recv, a_send, a_recv,
):
    me = lax.axis_index("member")
    lat = lax.axis_index("lat")
    south = lax.rem(lat + 1, NL)
    north = lax.rem(lat + NL - 1, NL)

    def peer(k):
        return lax.rem(me + k, NM)

    def source(k):
        return lax.rem(me + NM - k, NM)

    barrier = pltpu.get_barrier_semaphore()
    for k in range(1, NM):
        pl.semaphore_signal(barrier, inc=1, device_id={"member": peer(k)}, device_id_type=MESH)
    for there in (north, south):
        pl.semaphore_signal(barrier, inc=1, device_id={"lat": there}, device_id_type=MESH)
    pl.semaphore_wait(barrier, NM + 1)

    def halo(side, g):
        rows = pl.ds(pl.multiple_of(g * 8, 8), 8)
        src = xs.at[:, 0:4, rows, :] if side == 0 else xs.at[:, 4:8, rows, :]
        dst = (hb if side == 0 else ht).at[:, :, rows, :]
        return pltpu.make_async_remote_copy(
            src_ref=src, dst_ref=dst, send_sem=h_send.at[side, g], recv_sem=h_recv.at[side, g],
            device_id={"lat": north if side == 0 else south}, device_id_type=MESH,
        )

    @pl.loop(0, 8)
    def _(g):
        halo(0, g).start()
        halo(1, g).start()

    cells_at = iota((CELLS, CELLS), 0)
    for b in range(3):
        q = me + (b - 1)
        q_in = jnp.clip(q, 0, NM - 1)
        there = ((q >= 0) & (q < NM)).astype(jnp.int32).astype(F32)
        c_row = cell[lat, pl.ds(q_in, 1), :]
        p_row = prec[lat, pl.ds(q_in, 1), :] * there
        v_row = val[lat, pl.ds(q_in, 1), :] * p_row
        parts = []
        for r in (p_row, v_row):
            one = r.astype(BF16).astype(F32)
            two = (r - one).astype(BF16).astype(F32)
            parts += [one, two, r - one - two]
        lhs = jnp.concatenate(parts + [jnp.zeros((2, CELLS), F32)], axis=0).astype(BF16)
        hot = jnp.where(cells_at == c_row, 1.0, 0.0).astype(BF16)
        sums = dot(lhs, hot, NT)
        p_sum = sums[0:1] + sums[1:2] + sums[2:3]
        v_sum = sums[3:4] + sums[4:5] + sums[5:6]
        root = jnp.sqrt(p_sum)
        co[b, 0:1, :] = root
        co[b, 1:2, :] = jnp.where(p_sum > 0.0, v_sum / jnp.where(p_sum > 0.0, root, 1.0), 0.0)

    lane = iota((8, LON), 1)
    west_edge = lane == 0
    east_edge = lane == LON - 1
    lane1 = iota((8, 128), 1)
    halves = lane1 < 64
    evens = (lane1 & 32) == 0
    in_north = jnp.minimum(lat, 1).astype(F32)
    in_south = jnp.minimum(NL - 1 - lat, 1).astype(F32)

    def mask_row(r, state):
        if r < 0:
            return [s * in_north for s in state]
        if r >= ROWS:
            return [s * in_south for s in state]
        return state

    def slope(q):
        east = jnp.where(east_edge, 0.0, pltpu.roll(q, LON - 1, 1))
        west = jnp.where(west_edge, 0.0, pltpu.roll(q, 1, 1))
        return east - west

    half = 0.5 * DT

    def euler(states, r):
        h, u, v = states[r]
        above, below = states[r - 1], states[r + 1]
        spin = DT * (0.5 + ((lat * ROWS + r).astype(F32) * (1.0 / (NL * ROWS)) - 0.5))
        nh = h - half * (slope(u) + (below[2] - above[2]))
        nu = u - half * slope(h) + spin * v
        nv = v - half * (below[0] - above[0]) - spin * u
        return mask_row(r, [nh, nu, nv])

    for f in range(3):
        pk[f, 0, :, :] = jnp.zeros((LOC, CELLS), F32)
        pk[f, 9, :, :] = jnp.zeros((LOC, CELLS), F32)

    def obs_copy(g, k, mine):
        d = peer(k)
        src = pk.at[0, pl.ds(d, 3), pl.ds(pl.multiple_of(g * 8, 8), 8), :]
        owner = me if mine else source(k)
        dst = rh.at[:, pl.ds(pl.multiple_of(owner * LOC + g * 8, 8), 8), :]
        return pltpu.make_async_remote_copy(
            src_ref=src, dst_ref=dst, send_sem=o_send.at[g, k], recv_sem=o_recv.at[g, k],
            device_id={"member": d}, device_id_type=MESH,
        )

    far_first = (4, 2, 6, 3, 5, 1, 7)

    @pl.loop(0, 8)
    def _(g):
        halo(0, g).wait_recv()
        halo(1, g).wait_recv()
        rows = pl.ds(pl.multiple_of(g * 8, 8), 8)

        def start_row(r):
            if r < 0:
                vals = [ht[f, r + 4, rows, :] for f in range(3)]
            elif r >= ROWS:
                vals = [hb[f, r - ROWS, rows, :] for f in range(3)]
            else:
                vals = [xs[f, r, rows, :] for f in range(3)]
            return mask_row(r, vals)

        s0, m1, s1, m2, s2 = {}, {}, {}, {}, {}
        for r in range(-4, 12):
            s0[r] = start_row(r)
            if r - 1 >= -3:
                m1[r - 1] = euler(s0, r - 1)
            if r - 2 >= -2:
                nxt = euler(m1, r - 2)
                s1[r - 2] = [0.5 * (a + b) for a, b in zip(s0[r - 2], nxt)]
            if r - 3 >= -1:
                m2[r - 3] = euler(s1, r - 3)
            if r - 4 >= 0:
                nxt = euler(m2, r - 4)
                s2[r - 4] = [0.5 * (a + b) for a, b in zip(s1[r - 4], nxt)]
        for f in range(3):
            for t in range(2):
                for rg in range(2):
                    v = [s2[rg * 4 + j][f][:, t * 128 : (t + 1) * 128] for j in range(4)]
                    o = exchange_lanes(v, halves, evens)
                    for b in range(4):
                        pk[f, 1 + 4 * t + b, rows, rg * 128 : (rg + 1) * 128] = o[b]
        mine = pl.ds(pl.multiple_of(me * LOC + g * 8, 8), 8)
        for b in range(3):
            rh[b, mine, :] = pk[0, me + b, rows, :]
        for k in far_first:
            obs_copy(g, k, True).start()

    def field_copy(k, mine):
        d = peer(k)
        owner = me if mine else source(k)
        return pltpu.make_async_remote_copy(
            src_ref=pk.at[1:3, 1 + d, :, :],
            dst_ref=xf.at[:, pl.ds(pl.multiple_of(owner * LOC, LOC), LOC), :],
            send_sem=f_send.at[k], recv_sem=f_recv.at[k],
            device_id={"member": d}, device_id_type=MESH,
        )

    for k in far_first:
        field_copy(k, True).start()
    own = pl.ds(pl.multiple_of(me * LOC, LOC), LOC)
    for f in range(2):
        xf[f, own, :] = pk[1 + f, 1 + me, :, :]

    @pl.loop(0, 8)
    def _(g):
        for k in range(1, NM):
            obs_copy(g, k, False).wait_recv()

    for b in range(3):
        co[b, 2:3, :] = jnp.sum(rh[b], axis=0, keepdims=True) * (1.0 / ENS)
    c_at = iota((1, CELLS), 1)
    row_of = (c_at >> 5).astype(F32)
    col_of = (c_at & 31).astype(F32)

    def gram_copy(a, n):
        return pltpu.make_async_remote_copy(
            src_ref=gs.at[a, n], dst_ref=gr.at[a, n],
            send_sem=g_send.at[a, n], recv_sem=g_recv.at[a, n],
            device_id={"lat": north if a == 0 else south}, device_id_type=MESH,
        )

    def drive_copy(a):
        return pltpu.make_async_remote_copy(
            src_ref=ds_.at[a], dst_ref=dr.at[a],
            send_sem=g_send.at[a, 3], recv_sem=g_recv.at[a, 3],
            device_id={"lat": north if a == 0 else south}, device_id_type=MESH,
        )

    drive0 = None
    for a, offset in ((0, -1), (1, 1), (2, 0)):
        inside = {-1: in_north, 1: in_south, 0: 1.0}[offset]
        pushes = []
        for b in range(3):
            up = ((row_of - offset * ROWS) - 0.5 * (ROWS - 1)) / ROWS
            east = ((col_of + (b - 1) * 32) - 0.5 * 31) / 32
            t_root = jnp.exp(-0.25 * (up * up + east * east)) * inside
            s_w = t_root * co[b, 0:1, :]
            y_bar = co[b, 2:3, :]
            pushes.append(t_root * (co[b, 1:2, :] - y_bar * co[b, 0:1, :]))

            @pl.loop(0, ENS // 64)
            def _(n):
                r = pl.ds(pl.multiple_of(n * 64, 64), 64)
                s_h, s_l = split((rh[b, r, :] - y_bar) * s_w)
                sh[r, b * CELLS : (b + 1) * CELLS] = s_h
                sl[r, b * CELLS : (b + 1) * CELLS] = s_l

        drive = row_times(jnp.concatenate(pushes, axis=1), sh[...], sl[...], NT)
        if a < 2:
            ds_[a] = jnp.broadcast_to(drive, (8, ENS))
        else:
            drive0 = drive
        for n, (i, j) in enumerate(BLOCKS):
            ri, rj = slice(i * 256, (i + 1) * 256), slice(j * 256, (j + 1) * 256)
            acc = dot(sh[ri, :], sh[rj, :], NT) + dot(sh[ri, :], sl[rj, :], NT)
            acc = acc + dot(sl[ri, :], sh[rj, :], NT)
            if a < 2:
                gs[a, n] = acc
                gram_copy(a, n).start()
            else:
                g0[n] = acc
        if a < 2:
            drive_copy(a).start()

    for a in range(2):
        for n in range(3):
            gram_copy(a, n).wait_recv()
        drive_copy(a).wait_recv()
    drive = drive0 + dr[0, 0:1, :] + dr[1, 0:1, :]

    squares = jnp.zeros((8, 256), F32)
    for n, (i, j) in enumerate(BLOCKS):
        for part in range(4):
            r = slice(part * 64, (part + 1) * 64)
            tot = g0[n, r, :] + gr[0, n, r, :] + gr[1, n, r, :]
            if i == j:
                tot = tot + jnp.where(iota((64, 256), 0) + part * 64 == iota((64, 256), 1), ENS - 1.0, 0.0)
            g0[n, r, :] = tot
            sq = jnp.sum((tot * tot).reshape(8, 8, 256), axis=0)
            squares = squares + (sq if i == j else 2.0 * sq)
    fro = jnp.sqrt(jnp.sum(squares, axis=(0, 1), keepdims=True))
    inv_fro = 1.0 / fro

    def span(i):
        return slice(i * 256, (i + 1) * 256)

    def put(h, l, i, j, v):
        v_h, v_l = split(v)
        h[span(i), span(j)] = v_h
        l[span(i), span(j)] = v_l
        if i < j:
            h[span(j), span(i)] = v_h.T
            l[span(j), span(i)] = v_l.T

    def mul(a_h, a_l, b_h, b_l, i, j):
        acc = dot(a_h[span(i), :], b_h[:, span(j)]) + dot(a_h[span(i), :], b_l[:, span(j)])
        return acc + dot(a_l[span(i), :], b_h[:, span(j)])

    def eye(i, j, scale):
        if i != j:
            return 0.0
        return jnp.where(iota((256, 256), 0) == iota((256, 256), 1), scale, 0.0)

    def square(a_h, a_l):
        for i, j in BLOCKS:
            m = mf[span(i), span(j)]
            m2 = mul(a_h, a_l, a_h, a_l, i, j)
            put(bh, bl, i, j, m2)
            put(qh, ql, i, j, 0.0625 * m2 - 0.5625 * m)
            rf[span(i), span(j)] = (1.6875 * m2 - 2.4375 * m) + eye(i, j, 2.25)

    def pair_factor(to_h, to_l):
        for i, j in BLOCKS:
            put(to_h, to_l, i, j, rf[span(i), span(j)] + mul(bh, bl, qh, ql, i, j))

    def times(to_h, to_l, a_h, a_l, b_h, b_l):
        new = [mul(a_h, a_l, b_h, b_l, i, j) for i, j in BLOCKS]
        for (i, j), v in zip(BLOCKS, new):
            put(to_h, to_l, i, j, v)

    for n, (i, j) in enumerate(BLOCKS):
        scaled = g0[n] * inv_fro
        mf[span(i), span(j)] = scaled
        put(yh, yl, i, j, scaled)
    square(yh, yl)
    pair_factor(zh, zl)
    times(yh, yl, yh, yl, zh, zl)

    def step():
        for i, j in BLOCKS:
            m = mul(zh, zl, yh, yl, i, j)
            mf[span(i), span(j)] = m
            put(mh, ml, i, j, m)
        square(mh, ml)
        pair_factor(gh, gl)

    @pl.loop(0, 4)
    def _(n):
        step()
        times(yh, yl, yh, yl, gh, gl)
        times(zh, zl, gh, gl, zh, zl)

    step()
    times(zh, zl, gh, gl, zh, zl)

    for k in range(1, NM):
        field_copy(k, False).wait_recv()
    bars = []
    for f in range(3):
        ref = rh.at[1] if f == 0 else xf.at[f - 1]
        bar = co[1, 2:3, :] if f == 0 else jnp.sum(ref[...], axis=0, keepdims=True) * (1.0 / ENS)
        bars.append(bar)

        @pl.loop(0, ENS // 64)
        def _(n):
            r = pl.ds(pl.multiple_of(n * 64, 64), 64)
            x_h, x_l = split(ref[r, :] - bar)
            xh[r, f * CELLS : (f + 1) * CELLS] = x_h
            xl[r, f * CELLS : (f + 1) * CELLS] = x_l

    mean_weight = row_times(row_times(drive, zh[...], zl[...]), zh[...], zl[...]) * inv_fro
    bias = jnp.concatenate(bars, axis=1) + row_times(mean_weight, xh[...], xl[...])
    scale = math.sqrt(ENS - 1.0) / jnp.sqrt(fro)

    def analysis_copy(k, mine):
        d = peer(k)
        owner = me if mine else source(k)
        return pltpu.make_async_remote_copy(
            src_ref=ao.at[:, pl.ds(pl.multiple_of(d * LOC, LOC), LOC), :],
            dst_ref=ro.at[:, owner, :, :],
            send_sem=a_send.at[k], recv_sem=a_recv.at[k],
            device_id={"member": d}, device_id_type=MESH,
        )

    def analysed(d):
        r = pl.ds(pl.multiple_of(d * LOC, LOC), LOC)
        both = dot(jnp.concatenate([zh[r, :], zl[r, :]], axis=0), xh[...])
        acc = both[0:LOC] + both[LOC : 2 * LOC] + dot(zh[r, :], xl[...])
        return acc * scale + bias

    for k in far_first:
        d = peer(k)
        r = pl.ds(pl.multiple_of(d * LOC, LOC), LOC)
        res = analysed(d)
        for f in range(3):
            ao[f, r, :] = res[:, f * CELLS : (f + 1) * CELLS]
        analysis_copy(k, True).start()
    res = analysed(me)
    for f in range(3):
        ro[f, me, :, :] = res[:, f * CELLS : (f + 1) * CELLS]
    for k in range(1, NM):
        analysis_copy(k, False).wait_recv()

    @pl.loop(0, 8)
    def _(g):
        rows = pl.ds(pl.multiple_of(g * 8, 8), 8)
        for f in range(3):
            for t in range(2):
                for rg in range(2):
                    v = [ro[f, 4 * t + b, rows, rg * 128 : (rg + 1) * 128] for b in range(4)]
                    o = exchange_lanes(v, halves, evens)
                    for j in range(4):
                        out[f, rg * 4 + j, rows, t * 128 : (t + 1) * 128] = o[j]

    @pl.loop(0, 8)
    def _(g):
        halo(0, g).wait_send()
        halo(1, g).wait_send()
        for k in range(1, NM):
            obs_copy(g, k, True).wait_send()

    for k in range(1, NM):
        field_copy(k, True).wait_send()
        analysis_copy(k, True).wait_send()
    for a in range(2):
        for n in range(3):
            gram_copy(a, n).wait_send()
        drive_copy(a).wait_send()


def body(ensemble_state, obs_cell, obs_value, obs_prec):
    by_row = ensemble_state.transpose(0, 2, 1, 3)
    vmem = pl.BlockSpec(memory_space=pltpu.VMEM)
    half = pltpu.VMEM((ENS, ENS), BF16)
    full = pltpu.VMEM((ENS, ENS), F32)
    dma = pltpu.SemaphoreType.DMA
    analysed = pl.pallas_call(
        kernel,
        out_shape=jax.ShapeDtypeStruct((3, ROWS, LOC, LON), F32),
        in_specs=[vmem] * 4,
        out_specs=vmem,
        scratch_shapes=[
            pltpu.VMEM((3, 4, LOC, LON), F32),
            pltpu.VMEM((3, 4, LOC, LON), F32),
            pltpu.VMEM((3, 10, LOC, CELLS), F32),
            pltpu.VMEM((3, ENS, CELLS), F32),
            pltpu.VMEM((2, ENS, CELLS), F32),
            pltpu.VMEM((ENS, 768), BF16),
            pltpu.VMEM((ENS, 768), BF16),
            pltpu.VMEM((3, 256, 256), F32),
            pltpu.VMEM((2, 3, 256, 256), F32),
            pltpu.VMEM((2, 3, 256, 256), F32),
            pltpu.VMEM((2, 8, ENS), F32),
            pltpu.VMEM((2, 8, ENS), F32),
            pltpu.VMEM((3, 8, CELLS), F32),
        ]
        + [half] * 12
        + [full] * 2
        + [
            pltpu.VMEM((ENS, 768), BF16),
            pltpu.VMEM((ENS, 768), BF16),
            pltpu.VMEM((3, ENS, CELLS), F32),
            pltpu.VMEM((3, NM, LOC, CELLS), F32),
            dma((2, 8)),
            dma((2, 8)),
            dma((8, 8)),
            dma((8, 8)),
            dma((8,)),
            dma((8,)),
            dma((2, 4)),
            dma((2, 4)),
            dma((8,)),
            dma((8,)),
        ],
        compiler_params=pltpu.CompilerParams(
            collective_id=0, has_side_effects=True, vmem_limit_bytes=60 << 20
        ),
        name="letkf_cycle",
    )(by_row, obs_cell, obs_value, obs_prec)
    return analysed.transpose(0, 2, 1, 3)


def solution(mesh):
    in_specs = (P(None, "member", "lat", None), P(), P(), P())
    out_specs = P(None, "member", "lat", None)
    return jax.shard_map(body, mesh=mesh, in_specs=in_specs, out_specs=out_specs, check_vma=False)
```

profile of v0, /device:TPU:30, one launch (start us, length us, event | category | flops | bytes accessed | tf_op | source)
XLA Modules:
  0.0 105.2 jit_solution(16123921692634493769)
XLA Ops:
  0.0 3.0 %copy.8 = f32[3,64,8,256]{3,1,2,0:T(8,128)} copy(f32[3,64,8,256]{3,2,1,0:T(8,128)} %param.4) | data formatting | bytes 3145728 | tf_op args[0]
  3.0 98.7 %letkf_cycle.1 = f32[3,8,64,256]{3,2,1,0:T(8,128)} custom-call(f32[3,8,64,256]{3,2,1,0:T(8,128)} %bitcast.5, s32[16,8,256]{2,1,0:T(8,128)} %cell.1, f32[16,8,256]{2,1,0:T(8,128)} %val.1, f32[16,8,256]{2,1,0:T(8,128)} %prec.1), custom_call_target="tpu_custom_call" | custom-call | tf_op jit(solution)/shard_map/letkf_cycle/pallas_call | solution.py:450
  101.7 3.5 %copy.6 = f32[3,64,8,256]{3,2,1,0:T(8,128)} copy(f32[3,64,8,256]{3,1,2,0:T(8,128)} %bitcast.4) | data formatting | bytes 3145728 | tf_op jit(solution)/shard_map/transpose | solution.py:493
where the time goes:
time: 105 us
  Pallas kernels  98.7 us (94%)
  local copies, waits for them, and re-layouts  6.49 us (6%)
    pallas_call x1, Pallas kernels, body(): pl.pallas_call(kernel, out_shape=jax.ShapeDtypeStruct((3, ROWS, LOC, LON)...  98.7 us
    transpose x1, local copies, waits for them, and re-layouts, body(): return analysed.transpose(0, 2, 1, 3)  3.46 us
    unnamed x1, local copies, waits for them, and re-layouts  3.02 us

commit v1 on v0

--- a/solution.py
+++ b/solution.py
@@ -59,11 +59,10 @@
 
 
 def kernel(
-    xs, cell, val, prec, out,
-    ht, hb, pk, rh, xf, sh, sl, g0, gs, gr, ds_, dr, co,
-    yh, yl, zh, zl, mh, ml, bh, bl, qh, ql, gh, gl, mf, rf,
-    xh, xl, ao, ro,
-    h_send, h_recv, o_send, o_recv, f_send, f_recv, g_send, g_recv, a_send, a_recv,
+    x_in, cell_in, val_in, prec_in, ro, bo,
+    xn, cell, val, prec, xs, ht, hb, pk, rh, xf, sh, sl, s2h, s2l, g0, gs, gr, ds_, dr, co,
+    yh, yl, zh, zl, mh, ml, bh, bl, qh, ql, gh, gl, mf, rf, xh, xl, ao, bs,
+    in_sem, h_send, h_recv, o_send, o_recv, f_send, f_recv, g_send, g_recv, a_send, a_recv,
 ):
     me = lax.axis_index("member")
     lat = lax.axis_index("lat")
@@ -76,12 +75,36 @@
     def source(k):
         return lax.rem(me + NM - k, NM)
 
+    def state_in(g):
+        rows = pl.ds(pl.multiple_of(g * 8, 8), 8)
+        return pltpu.make_async_copy(x_in.at[:, rows], xn.at[:, rows], in_sem.at[g])
+
+    obs_in = [
+        pltpu.make_async_copy(a.at[lat], b, in_sem.at[8 + i])
+        for i, (a, b) in enumerate(((cell_in, cell), (val_in, val), (prec_in, prec)))
+    ]
+    for g in range(8):
+        state_in(g).start()
+    for c in obs_in:
+        c.start()
     barrier = pltpu.get_barrier_semaphore()
     for k in range(1, NM):
         pl.semaphore_signal(barrier, inc=1, device_id={"member": peer(k)}, device_id_type=MESH)
     for there in (north, south):
         pl.semaphore_signal(barrier, inc=1, device_id={"lat": there}, device_id_type=MESH)
-    pl.semaphore_wait(barrier, NM + 1)
+
+    with jax.named_scope("load"):
+
+        @pl.loop(0, 8)
+        def _(g):
+            state_in(g).wait()
+            rows = pl.ds(pl.multiple_of(g * 8, 8), 8)
+            for f in range(3):
+                for r in range(ROWS):
+                    xs[f, r, rows, :] = xn[f, rows, r, :]
+
+    with jax.named_scope("barrier"):
+        pl.semaphore_wait(barrier, NM + 1)
 
     def halo(side, g):
         rows = pl.ds(pl.multiple_of(g * 8, 8), 8)
@@ -97,14 +120,16 @@
         halo(0, g).start()
         halo(1, g).start()
 
+    for c in obs_in:
+        c.wait()
     cells_at = iota((CELLS, CELLS), 0)
     for b in range(3):
         q = me + (b - 1)
         q_in = jnp.clip(q, 0, NM - 1)
         there = ((q >= 0) & (q < NM)).astype(jnp.int32).astype(F32)
-        c_row = cell[lat, pl.ds(q_in, 1), :]
-        p_row = prec[lat, pl.ds(q_in, 1), :] * there
-        v_row = val[lat, pl.ds(q_in, 1), :] * p_row
+        c_row = cell[pl.ds(q_in, 1), :]
+        p_row = prec[pl.ds(q_in, 1), :] * there
+        v_row = val[pl.ds(q_in, 1), :] * p_row
         parts = []
         for r in (p_row, v_row):
             one = r.astype(BF16).astype(F32)
@@ -151,17 +176,29 @@
         nv = v - half * (below[0] - above[0]) - spin * u
         return mask_row(r, [nh, nu, nv])
 
-    for f in range(3):
-        pk[f, 0, :, :] = jnp.zeros((LOC, CELLS), F32)
-        pk[f, 9, :, :] = jnp.zeros((LOC, CELLS), F32)
+    pk[0, 0, :, :] = jnp.zeros((LOC, CELLS), F32)
+
+    @pl.when(me == NM - 1)
+    def _():
+        rh[2] = jnp.zeros((ENS, CELLS), F32)
 
     def obs_copy(g, k, mine):
         d = peer(k)
-        src = pk.at[0, pl.ds(d, 3), pl.ds(pl.multiple_of(g * 8, 8), 8), :]
+        src = pk.at[0, pl.ds(d, 2), pl.ds(pl.multiple_of(g * 8, 8), 8), :]
         owner = me if mine else source(k)
-        dst = rh.at[:, pl.ds(pl.multiple_of(owner * LOC + g * 8, 8), 8), :]
+        dst = rh.at[0:2, pl.ds(pl.multiple_of(owner * LOC + g * 8, 8), 8), :]
         return pltpu.make_async_remote_copy(
             src_ref=src, dst_ref=dst, send_sem=o_send.at[g, k], recv_sem=o_recv.at[g, k],
+            device_id={"member": d}, device_id_type=MESH,
+        )
+
+    def east_copy(k, mine):
+        d = peer(k)
+        owner = me if mine else source(k)
+        return pltpu.make_async_remote_copy(
+            src_ref=pk.at[0, d + 2, :, :],
+            dst_ref=rh.at[2, pl.ds(pl.multiple_of(owner * LOC, LOC), LOC), :],
+            send_sem=o_send.at[8, k], recv_sem=o_recv.at[8, k],
             device_id={"member": d}, device_id_type=MESH,
         )
 
@@ -203,7 +240,7 @@
                     for b in range(4):
                         pk[f, 1 + 4 * t + b, rows, rg * 128 : (rg + 1) * 128] = o[b]
         mine = pl.ds(pl.multiple_of(me * LOC + g * 8, 8), 8)
-        for b in range(3):
+        for b in range(2):
             rh[b, mine, :] = pk[0, me + b, rows, :]
         for k in far_first:
             obs_copy(g, k, True).start()
@@ -219,88 +256,149 @@
         )
 
     for k in far_first:
+
+        @pl.when(peer(k) < NM - 1)
+        def _():
+            east_copy(k, True).start()
+
+    for k in far_first:
         field_copy(k, True).start()
     own = pl.ds(pl.multiple_of(me * LOC, LOC), LOC)
     for f in range(2):
         xf[f, own, :] = pk[1 + f, 1 + me, :, :]
 
-    @pl.loop(0, 8)
-    def _(g):
-        for k in range(1, NM):
-            obs_copy(g, k, False).wait_recv()
-
-    for b in range(3):
-        co[b, 2:3, :] = jnp.sum(rh[b], axis=0, keepdims=True) * (1.0 / ENS)
+    @pl.when(me < NM - 1)
+    def _():
+        rh[2, own, :] = pk[0, me + 2, :, :]
+
+    with jax.named_scope("obs01"):
+
+        @pl.loop(0, 8)
+        def _(g):
+            for k in range(1, NM):
+                obs_copy(g, k, False).wait_recv()
+
+    odd = lax.rem(lat, 2)
+    first_peer = lax.rem(lat + NL - 1 + 2 * odd, NL)
+    second_peer = lax.rem(lat + NL + 1 - 2 * odd, NL)
+    odd_f = odd.astype(F32)
+    shifts = (2.0 * odd_f - 1.0, 1.0 - 2.0 * odd_f, 0.0)
+    insides = (
+        in_north * (1.0 - odd_f) + in_south * odd_f,
+        in_south * (1.0 - odd_f) + in_north * odd_f,
+        1.0,
+    )
     c_at = iota((1, CELLS), 1)
     row_of = (c_at >> 5).astype(F32)
     col_of = (c_at & 31).astype(F32)
 
-    def gram_copy(a, n):
+    def remote_gram(a, src, dst, n):
         return pltpu.make_async_remote_copy(
-            src_ref=gs.at[a, n], dst_ref=gr.at[a, n],
-            send_sem=g_send.at[a, n], recv_sem=g_recv.at[a, n],
-            device_id={"lat": north if a == 0 else south}, device_id_type=MESH,
+            src_ref=src, dst_ref=dst, send_sem=g_send.at[a, n], recv_sem=g_recv.at[a, n],
+            device_id={"lat": first_peer if a == 0 else second_peer}, device_id_type=MESH,
         )
 
+    low, top = slice(128, 256), slice(0, 128)
+
+    def gram_copies(a, n):
+        if n == 1:
+            return [remote_gram(a, gs.at[a, 1], gr.at[a, 1], 2)]
+        at = 0 if n == 0 else 3
+        return [
+            remote_gram(a, gs.at[a, n, top, :], gr.at[a, n, top, :], at),
+            remote_gram(a, gs.at[a, n, low, low], gr.at[a, n, low, low], at + 1),
+        ]
+
     def drive_copy(a):
-        return pltpu.make_async_remote_copy(
-            src_ref=ds_.at[a], dst_ref=dr.at[a],
-            send_sem=g_send.at[a, 3], recv_sem=g_recv.at[a, 3],
-            device_id={"lat": north if a == 0 else south}, device_id_type=MESH,
-        )
-
-    drive0 = None
-    for a, offset in ((0, -1), (1, 1), (2, 0)):
-        inside = {-1: in_north, 1: in_south, 0: 1.0}[offset]
-        pushes = []
-        for b in range(3):
-            up = ((row_of - offset * ROWS) - 0.5 * (ROWS - 1)) / ROWS
-            east = ((col_of + (b - 1) * 32) - 0.5 * 31) / 32
-            t_root = jnp.exp(-0.25 * (up * up + east * east)) * inside
-            s_w = t_root * co[b, 0:1, :]
-            y_bar = co[b, 2:3, :]
-            pushes.append(t_root * (co[b, 1:2, :] - y_bar * co[b, 0:1, :]))
-
-            @pl.loop(0, ENS // 64)
-            def _(n):
-                r = pl.ds(pl.multiple_of(n * 64, 64), 64)
-                s_h, s_l = split((rh[b, r, :] - y_bar) * s_w)
-                sh[r, b * CELLS : (b + 1) * CELLS] = s_h
-                sl[r, b * CELLS : (b + 1) * CELLS] = s_l
-
-        drive = row_times(jnp.concatenate(pushes, axis=1), sh[...], sl[...], NT)
-        if a < 2:
-            ds_[a] = jnp.broadcast_to(drive, (8, ENS))
-        else:
-            drive0 = drive
-        for n, (i, j) in enumerate(BLOCKS):
-            ri, rj = slice(i * 256, (i + 1) * 256), slice(j * 256, (j + 1) * 256)
-            acc = dot(sh[ri, :], sh[rj, :], NT) + dot(sh[ri, :], sl[rj, :], NT)
-            acc = acc + dot(sl[ri, :], sh[rj, :], NT)
+        return remote_gram(a, ds_.at[a], dr.at[a], 5)
+
+    def member_mean(b):
+        co[b, 2:3, :] = jnp.sum(rh[b], axis=0, keepdims=True) * (1.0 / ENS)
+
+    def weigh(a, b, to_h, to_l, at):
+        up = ((row_of - shifts[a] * ROWS) - 0.5 * (ROWS - 1)) / ROWS
+        east = ((col_of + (b - 1) * 32) - 0.5 * 31) / 32
+        t_root = jnp.exp(-0.25 * (up * up + east * east)) * insides[a]
+        s_w = t_root * co[b, 0:1, :]
+        y_bar = co[b, 2:3, :]
+
+        @pl.loop(0, ENS // 64)
+        def _(n):
+            r = pl.ds(pl.multiple_of(n * 64, 64), 64)
+            s_h, s_l = split((rh[b, r, :] - y_bar) * s_w)
+            to_h[r, at : at + CELLS] = s_h
+            to_l[r, at : at + CELLS] = s_l
+
+        return t_root * (co[b, 1:2, :] - y_bar * co[b, 0:1, :])
+
+    def products(h, l, i, j):
+        ri, rj = slice(i * 256, (i + 1) * 256), slice(j * 256, (j + 1) * 256)
+        acc = dot(h[ri, :], h[rj, :], NT) + dot(h[ri, :], l[rj, :], NT)
+        return acc + dot(l[ri, :], h[rj, :], NT)
+
+    for b in range(2):
+        member_mean(b)
+    drives = []
+    with jax.named_scope("gram01"):
+        for a in range(3):
+            push = [weigh(a, b, sh, sl, b * CELLS) for b in range(2)]
+            drives.append(row_times(jnp.concatenate(push, axis=1), sh[...], sl[...], NT))
+            for n, (i, j) in enumerate(BLOCKS):
+                if a < 2:
+                    gs[a, n] = products(sh, sl, i, j)
+                else:
+                    g0[n] = products(sh, sl, i, j)
+
+    with jax.named_scope("obs2"):
+
+        @pl.when(me < NM - 1)
+        def _():
+            for k in range(1, NM):
+                east_copy(k, False).wait_recv()
+
+    member_mean(2)
+    with jax.named_scope("gram2"):
+        for a in range(3):
+            push = weigh(a, 2, s2h, s2l, 0)
+            for n, (i, j) in enumerate(BLOCKS):
+                if a < 2:
+                    gs[a, n] = gs[a, n] + products(s2h, s2l, i, j)
+                    for c in gram_copies(a, n):
+                        c.start()
+                else:
+                    g0[n] = g0[n] + products(s2h, s2l, i, j)
+            drives[a] = drives[a] + row_times(push, s2h[...], s2l[...], NT)
             if a < 2:
-                gs[a, n] = acc
-                gram_copy(a, n).start()
-            else:
-                g0[n] = acc
-        if a < 2:
-            drive_copy(a).start()
-
-    for a in range(2):
-        for n in range(3):
-            gram_copy(a, n).wait_recv()
-        drive_copy(a).wait_recv()
-    drive = drive0 + dr[0, 0:1, :] + dr[1, 0:1, :]
-
-    squares = jnp.zeros((8, 256), F32)
+                ds_[a] = jnp.broadcast_to(drives[a], (8, ENS))
+                drive_copy(a).start()
+
+    with jax.named_scope("gwait"):
+        for a in range(2):
+            for n in range(3):
+                for c in gram_copies(a, n):
+                    c.wait_recv()
+            drive_copy(a).wait_recv()
+    drive = drives[2] + dr[0, 0:1, :] + dr[1, 0:1, :]
+
+    squares = jnp.zeros((8, 128), F32)
     for n, (i, j) in enumerate(BLOCKS):
         for part in range(4):
-            r = slice(part * 64, (part + 1) * 64)
-            tot = g0[n, r, :] + gr[0, n, r, :] + gr[1, n, r, :]
-            if i == j:
-                tot = tot + jnp.where(iota((64, 256), 0) + part * 64 == iota((64, 256), 1), ENS - 1.0, 0.0)
-            g0[n, r, :] = tot
-            sq = jnp.sum((tot * tot).reshape(8, 8, 256), axis=0)
-            squares = squares + (sq if i == j else 2.0 * sq)
+            if i == j and part >= 2:
+                lanes = ((part * 64, 128),)
+            else:
+                lanes = ((0, 0), (0, 128))
+            for _unused, c0 in lanes:
+                r, c = slice(part * 64, (part + 1) * 64), slice(c0, c0 + 128)
+                tot = g0[n, r, c] + gr[0, n, r, c] + gr[1, n, r, c]
+                if i == j:
+                    on = iota((64, 128), 0) + part * 64 == iota((64, 128), 1) + c0
+                    tot = tot + jnp.where(on, ENS - 1.0, 0.0)
+                g0[n, r, c] = tot
+                sq = jnp.sum((tot * tot).reshape(8, 8, 128), axis=0)
+                twice = i != j or (part < 2 and c0 == 128)
+                squares = squares + (2.0 * sq if twice else sq)
+        if i == j:
+            g0[n, low, top] = g0[n, top, low].T
     fro = jnp.sqrt(jnp.sum(squares, axis=(0, 1), keepdims=True))
     inv_fro = 1.0 / fro
 
@@ -341,6 +439,21 @@
         for (i, j), v in zip(BLOCKS, new):
             put(to_h, to_l, i, j, v)
 
+    def take_states(f):
+        ref = rh.at[1] if f == 0 else xf.at[f - 1]
+        if f == 0:
+            bar = co[1, 2:3, :]
+        else:
+            bar = jnp.sum(ref[...], axis=0, keepdims=True) * (1.0 / ENS)
+        bs[0:1, f * CELLS : (f + 1) * CELLS] = bar
+
+        @pl.loop(0, ENS // 64)
+        def _(n):
+            r = pl.ds(pl.multiple_of(n * 64, 64), 64)
+            x_h, x_l = split(ref[r, :] - bar)
+            xh[r, f * CELLS : (f + 1) * CELLS] = x_h
+            xl[r, f * CELLS : (f + 1) * CELLS] = x_l
+
     for n, (i, j) in enumerate(BLOCKS):
         scaled = g0[n] * inv_fro
         mf[span(i), span(j)] = scaled
@@ -357,32 +470,24 @@
         square(mh, ml)
         pair_factor(gh, gl)
 
-    @pl.loop(0, 4)
-    def _(n):
+    with jax.named_scope("ns"):
+
+        @pl.loop(0, 4)
+        def _(n):
+            step()
+            times(yh, yl, yh, yl, gh, gl)
+            times(zh, zl, gh, gl, zh, zl)
+
+    with jax.named_scope("fields"):
+        for k in range(1, NM):
+            field_copy(k, False).wait_recv()
+    with jax.named_scope("states"):
+        for f in range(3):
+            take_states(f)
+
+    with jax.named_scope("ns5"):
         step()
-        times(yh, yl, yh, yl, gh, gl)
         times(zh, zl, gh, gl, zh, zl)
-
-    step()
-    times(zh, zl, gh, gl, zh, zl)
-
-    for k in range(1, NM):
-        field_copy(k, False).wait_recv()
-    bars = []
-    for f in range(3):
-        ref = rh.at[1] if f == 0 else xf.at[f - 1]
-        bar = co[1, 2:3, :] if f == 0 else jnp.sum(ref[...], axis=0, keepdims=True) * (1.0 / ENS)
-        bars.append(bar)
-
-        @pl.loop(0, ENS // 64)
-        def _(n):
-            r = pl.ds(pl.multiple_of(n * 64, 64), 64)
-            x_h, x_l = split(ref[r, :] - bar)
-            xh[r, f * CELLS : (f + 1) * CELLS] = x_h
-            xl[r, f * CELLS : (f + 1) * CELLS] = x_l
-
-    mean_weight = row_times(row_times(drive, zh[...], zl[...]), zh[...], zl[...]) * inv_fro
-    bias = jnp.concatenate(bars, axis=1) + row_times(mean_weight, xh[...], xl[...])
     scale = math.sqrt(ENS - 1.0) / jnp.sqrt(fro)
 
     def analysis_copy(k, mine):
@@ -391,7 +496,7 @@
         return pltpu.make_async_remote_copy(
             src_ref=ao.at[:, pl.ds(pl.multiple_of(d * LOC, LOC), LOC), :],
             dst_ref=ro.at[:, owner, :, :],
-            send_sem=a_send.at[k], recv_sem=a_recv.at[k],
+            send_sem=a_send.at[0, k], recv_sem=a_recv.at[0, k],
             device_id={"member": d}, device_id_type=MESH,
         )
 
@@ -399,7 +504,17 @@
         r = pl.ds(pl.multiple_of(d * LOC, LOC), LOC)
         both = dot(jnp.concatenate([zh[r, :], zl[r, :]], axis=0), xh[...])
         acc = both[0:LOC] + both[LOC : 2 * LOC] + dot(zh[r, :], xl[...])
-        return acc * scale + bias
+        return acc * scale
+
+    def bias_copy(k, mine):
+        d = peer(k)
+        owner = me if mine else source(k)
+        return pltpu.make_async_remote_copy(
+            src_ref=bs, dst_ref=bo.at[owner],
+            send_sem=a_send.at[1, k], recv_sem=a_recv.at[1, k],
+            device_id={"member": d}, device_id_type=MESH,
+        )
+
 
     for k in far_first:
         d = peer(k)
@@ -411,19 +526,16 @@
     res = analysed(me)
     for f in range(3):
         ro[f, me, :, :] = res[:, f * CELLS : (f + 1) * CELLS]
-    for k in range(1, NM):
-        analysis_copy(k, False).wait_recv()
-
-    @pl.loop(0, 8)
-    def _(g):
-        rows = pl.ds(pl.multiple_of(g * 8, 8), 8)
-        for f in range(3):
-            for t in range(2):
-                for rg in range(2):
-                    v = [ro[f, 4 * t + b, rows, rg * 128 : (rg + 1) * 128] for b in range(4)]
-                    o = exchange_lanes(v, halves, evens)
-                    for j in range(4):
-                        out[f, rg * 4 + j, rows, t * 128 : (t + 1) * 128] = o[j]
+    mean_weight = row_times(row_times(drive, zh[...], zl[...]), zh[...], zl[...]) * inv_fro
+    bias = bs[0:1, :] + row_times(mean_weight, xh[...], xl[...])
+    bs[...] = jnp.broadcast_to(bias, (8, 768))
+    bo[me] = jnp.broadcast_to(bias, (8, 768))
+    for k in far_first:
+        bias_copy(k, True).start()
+    with jax.named_scope("out"):
+        for k in range(1, NM):
+            analysis_copy(k, False).wait_recv()
+            bias_copy(k, False).wait_recv()
 
     @pl.loop(0, 8)
     def _(g):
@@ -433,33 +545,68 @@
             obs_copy(g, k, True).wait_send()
 
     for k in range(1, NM):
+
+        @pl.when(peer(k) < NM - 1)
+        def _():
+            east_copy(k, True).wait_send()
+
+    for k in range(1, NM):
         field_copy(k, True).wait_send()
         analysis_copy(k, True).wait_send()
+        bias_copy(k, True).wait_send()
     for a in range(2):
         for n in range(3):
-            gram_copy(a, n).wait_send()
+            for c in gram_copies(a, n):
+                c.wait_send()
         drive_copy(a).wait_send()
 
 
+def unpack(ro, bo, out):
+    lane1 = iota((8, 128), 1)
+    halves = lane1 < 64
+    evens = (lane1 & 32) == 0
+    for f in range(3):
+        for t in range(2):
+            for rg in range(2):
+                at = f * CELLS + rg * 128
+                v = [
+                    ro[f, 4 * t + b, :, rg * 128 : (rg + 1) * 128] + bo[4 * t + b, :, at : at + 128]
+                    for b in range(4)
+                ]
+                o = exchange_lanes(v, halves, evens)
+                for j in range(4):
+                    out[f, :, rg * 4 + j, t * 128 : (t + 1) * 128] = o[j]
+
+
 def body(ensemble_state, obs_cell, obs_value, obs_prec):
-    by_row = ensemble_state.transpose(0, 2, 1, 3)
     vmem = pl.BlockSpec(memory_space=pltpu.VMEM)
+    anywhere = pl.BlockSpec(memory_space=pltpu.HBM)
     half = pltpu.VMEM((ENS, ENS), BF16)
     full = pltpu.VMEM((ENS, ENS), F32)
     dma = pltpu.SemaphoreType.DMA
-    analysed = pl.pallas_call(
+    received, biases = pl.pallas_call(
         kernel,
-        out_shape=jax.ShapeDtypeStruct((3, ROWS, LOC, LON), F32),
-        in_specs=[vmem] * 4,
-        out_specs=vmem,
+        out_shape=(
+            jax.ShapeDtypeStruct((3, NM, LOC, CELLS), F32),
+            jax.ShapeDtypeStruct((NM, 8, 768), F32),
+        ),
+        in_specs=[anywhere] * 4,
+        out_specs=(vmem, vmem),
         scratch_shapes=[
+            pltpu.VMEM((3, LOC, ROWS, LON), F32),
+            pltpu.VMEM((8, 256), jnp.int32),
+            pltpu.VMEM((8, 256), F32),
+            pltpu.VMEM((8, 256), F32),
+            pltpu.VMEM((3, ROWS, LOC, LON), F32),
             pltpu.VMEM((3, 4, LOC, LON), F32),
             pltpu.VMEM((3, 4, LOC, LON), F32),
             pltpu.VMEM((3, 10, LOC, CELLS), F32),
             pltpu.VMEM((3, ENS, CELLS), F32),
             pltpu.VMEM((2, ENS, CELLS), F32),
-            pltpu.VMEM((ENS, 768), BF16),
-            pltpu.VMEM((ENS, 768), BF16),
+            pltpu.VMEM((ENS, 512), BF16),
+            pltpu.VMEM((ENS, 512), BF16),
+            pltpu.VMEM((ENS, 256), BF16),
+            pltpu.VMEM((ENS, 256), BF16),
             pltpu.VMEM((3, 256, 256), F32),
             pltpu.VMEM((2, 3, 256, 256), F32),
             pltpu.VMEM((2, 3, 256, 256), F32),
@@ -473,24 +620,36 @@
             pltpu.VMEM((ENS, 768), BF16),
             pltpu.VMEM((ENS, 768), BF16),
             pltpu.VMEM((3, ENS, CELLS), F32),
-            pltpu.VMEM((3, NM, LOC, CELLS), F32),
+            pltpu.VMEM((8, 768), F32),
+            dma((11,)),
             dma((2, 8)),
             dma((2, 8)),
-            dma((8, 8)),
-            dma((8, 8)),
+            dma((9, 8)),
+            dma((9, 8)),
             dma((8,)),
             dma((8,)),
-            dma((2, 4)),
-            dma((2, 4)),
-            dma((8,)),
-            dma((8,)),
+            dma((2, 6)),
+            dma((2, 6)),
+            dma((2, 8)),
+            dma((2, 8)),
         ],
         compiler_params=pltpu.CompilerParams(
-            collective_id=0, has_side_effects=True, vmem_limit_bytes=60 << 20
+            collective_id=0, has_side_effects=True, vmem_limit_bytes=40 << 20
         ),
         name="letkf_cycle",
-    )(by_row, obs_cell, obs_value, obs_prec)
-    return analysed.transpose(0, 2, 1, 3)
+    )(ensemble_state, obs_cell, obs_value, obs_prec)
+    return pl.pallas_call(
+        unpack,
+        grid=(8,),
+        out_shape=jax.ShapeDtypeStruct((3, LOC, ROWS, LON), F32),
+        in_specs=[
+            pl.BlockSpec((3, NM, 8, CELLS), lambda g: (0, 0, g, 0)),
+            pl.BlockSpec((NM, 8, 768), lambda g: (0, 0, 0)),
+        ],
+        out_specs=pl.BlockSpec((3, 8, ROWS, LON), lambda g: (0, g, 0, 0)),
+        compiler_params=pltpu.CompilerParams(vmem_limit_bytes=16 << 20),
+        name="unpack",
+    )(received, biases)
 
 
 def solution(mesh):

time: 105 us -> 98.2 us (0.935)
  the two profiles are of different devices: /device:TPU:30 before, /device:TPU:0 now
where the time goes in v1:
time: 98.2 us; the launch traced here: 98 us
  Pallas kernels  93.9 us (96%)
  local copies, waits for them, and re-layouts  4.12 us (4%)
    pallas_call x1, Pallas kernels, body(): pl.pallas_call(kernel, out_shape=(jax.ShapeDtypeStruct((3, NM, LOC, CELLS...  89.8 us
    unnamed x8, local copies, waits for them, and re-layouts  4.12 us
    pallas_call x1, Pallas kernels, body(): pl.pallas_call(unpack, grid=(8,), out_shape=jax.ShapeDtypeStruct((3, LOC,...  4.08 us

profile of v1, /device:TPU:0, one launch (start us, length us, event | category | flops | bytes accessed | tf_op | source)
XLA Modules:
  0.0 98.0 jit_solution(8356353351975825067)
XLA Ops:
  0.0 0.0 copy-start
  0.0 1.4 %copy-done = f32[3,64,8,256]{3,2,1,0:T(8,128)S(1)} copy-done((f32[3,64,8,256]{3,2,1,0:T(8,128)S(1)}, f32[3,64,8,256]{3,2,1,0:T(8,128)}, u32[]{:S(2)}) %copy-start) | copy-done | bytes 1572888
  1.4 0.0 copy-start.1
  1.4 0.9 copy-done.1
  2.3 0.0 copy-start.2
  2.3 0.9 copy-done.2
  3.2 0.0 copy-start.3
  3.2 0.9 copy-done.3
  4.1 89.8 %letkf_cycle.1 = (f32[3,8,64,256]{3,2,1,0:T(8,128)S(1)}, f32[8,8,768]{2,1,0:T(8,128)S(1)}) custom-call(f32[3,64,8,256]{3,2,1,0:T(8,128)S(1)} %copy-done, s32[16,8,256]{2,1,0:T(8,128)S(1)} %copy-done.1, f32[16,8,256]{2,1,0:T(8,128)S(1)} %copy-done.2, f32[16,8,256]{2,1,0:T(8,128)S(1)} %copy-done.3), custom_call_target="tpu_custom_call" | custom-call | tf_op jit(solution)/shard_map/letkf_cycle/pallas_call | solution.py:587
  93.9 4.1 %unpack.1 = f32[3,64,8,256]{3,2,1,0:T(8,128)} custom-call(f32[3,8,64,256]{3,2,1,0:T(8,128)S(1)} %get-tuple-element.7.ro, f32[8,8,768]{2,1,0:T(8,128)S(1)} %get-tuple-element.8.bo), custom_call_target="tpu_custom_call" | custom-call | tf_op jit(solution)/shard_map/unpack/pallas_call | solution.py:641
Async XLA Ops:
  0.0 1.4 %copy-start = (f32[3,64,8,256]{3,2,1,0:T(8,128)S(1)}, f32[3,64,8,256]{3,2,1,0:T(8,128)}, u32[]{:S(2)}) copy-start(f32[3,64,8,256]{3,2,1,0:T(8,128)} %x_in.1) | copy-start | bytes 4718596
  1.4 0.9 copy-start.1
  2.3 0.9 copy-start.2
  3.2 0.9 copy-start.3

commit v2 on v1

--- a/solution.py
+++ b/solution.py
@@ -115,10 +115,25 @@
             device_id={"lat": north if side == 0 else south}, device_id_type=MESH,
         )
 
-    @pl.loop(0, 8)
-    def _(g):
-        halo(0, g).start()
-        halo(1, g).start()
+    has_north, has_south = lat > 0, lat < NL - 1
+
+    @pl.when(has_north)
+    def _():
+        for g in range(8):
+            halo(0, g).start()
+
+    @pl.when(has_south)
+    def _():
+        for g in range(8):
+            halo(1, g).start()
+
+    @pl.when(lat == 0)
+    def _():
+        ht[...] = jnp.zeros((3, 4, LOC, LON), F32)
+
+    @pl.when(lat == NL - 1)
+    def _():
+        hb[...] = jnp.zeros((3, 4, LOC, LON), F32)
 
     for c in obs_in:
         c.wait()
@@ -206,8 +221,15 @@
 
     @pl.loop(0, 8)
     def _(g):
-        halo(0, g).wait_recv()
-        halo(1, g).wait_recv()
+
+        @pl.when(has_south)
+        def _():
+            halo(0, g).wait_recv()
+
+        @pl.when(has_north)
+        def _():
+            halo(1, g).wait_recv()
+
         rows = pl.ds(pl.multiple_of(g * 8, 8), 8)
 
         def start_row(r):
@@ -217,7 +239,7 @@
                 vals = [hb[f, r - ROWS, rows, :] for f in range(3)]
             else:
                 vals = [xs[f, r, rows, :] for f in range(3)]
-            return mask_row(r, vals)
+            return vals
 
         s0, m1, s1, m2, s2 = {}, {}, {}, {}, {}
         for r in range(-4, 12):
@@ -261,8 +283,6 @@
         def _():
             east_copy(k, True).start()
 
-    for k in far_first:
-        field_copy(k, True).start()
     own = pl.ds(pl.multiple_of(me * LOC, LOC), LOC)
     for f in range(2):
         xf[f, own, :] = pk[1 + f, 1 + me, :, :]
@@ -299,6 +319,18 @@
         )
 
     low, top = slice(128, 256), slice(0, 128)
+    has_far = has_north & has_south
+
+    def towards(a, act):
+        if a == 0:
+            pl.when(has_far)(act)
+        else:
+            act()
+
+    @pl.when((lat == 0) | (lat == NL - 1))
+    def _():
+        gr[0] = jnp.zeros((3, 256, 256), F32)
+        dr[0] = jnp.zeros((8, ENS), F32)
 
     def gram_copies(a, n):
         if n == 1:
@@ -363,21 +395,32 @@
             for n, (i, j) in enumerate(BLOCKS):
                 if a < 2:
                     gs[a, n] = gs[a, n] + products(s2h, s2l, i, j)
-                    for c in gram_copies(a, n):
-                        c.start()
+
+                    def send(a=a, n=n):
+                        for c in gram_copies(a, n):
+                            c.start()
+
+                    towards(a, send)
                 else:
                     g0[n] = g0[n] + products(s2h, s2l, i, j)
             drives[a] = drives[a] + row_times(push, s2h[...], s2l[...], NT)
             if a < 2:
                 ds_[a] = jnp.broadcast_to(drives[a], (8, ENS))
-                drive_copy(a).start()
+                towards(a, lambda a=a: drive_copy(a).start())
+            if a == 1:
+                for k in far_first:
+                    field_copy(k, True).start()
 
     with jax.named_scope("gwait"):
         for a in range(2):
-            for n in range(3):
-                for c in gram_copies(a, n):
-                    c.wait_recv()
-            drive_copy(a).wait_recv()
+
+            def arrive(a=a):
+                for n in range(3):
+                    for c in gram_copies(a, n):
+                        c.wait_recv()
+                drive_copy(a).wait_recv()
+
+            towards(a, arrive)
     drive = drives[2] + dr[0, 0:1, :] + dr[1, 0:1, :]
 
     squares = jnp.zeros((8, 128), F32)
@@ -539,8 +582,15 @@
 
     @pl.loop(0, 8)
     def _(g):
-        halo(0, g).wait_send()
-        halo(1, g).wait_send()
+
+        @pl.when(has_north)
+        def _():
+            halo(0, g).wait_send()
+
+        @pl.when(has_south)
+        def _():
+            halo(1, g).wait_send()
+
         for k in range(1, NM):
             obs_copy(g, k, True).wait_send()
 
@@ -555,27 +605,44 @@
         analysis_copy(k, True).wait_send()
         bias_copy(k, True).wait_send()
     for a in range(2):
-        for n in range(3):
-            for c in gram_copies(a, n):
-                c.wait_send()
-        drive_copy(a).wait_send()
-
-
-def unpack(ro, bo, out):
+
+        def left(a=a):
+            for n in range(3):
+                for c in gram_copies(a, n):
+                    c.wait_send()
+            drive_copy(a).wait_send()
+
+        towards(a, left)
+
+
+def unpack(ro, bo, out, held, sem):
     lane1 = iota((8, 128), 1)
     halves = lane1 < 64
     evens = (lane1 & 32) == 0
-    for f in range(3):
-        for t in range(2):
-            for rg in range(2):
-                at = f * CELLS + rg * 128
-                v = [
-                    ro[f, 4 * t + b, :, rg * 128 : (rg + 1) * 128] + bo[4 * t + b, :, at : at + 128]
-                    for b in range(4)
-                ]
-                o = exchange_lanes(v, halves, evens)
-                for j in range(4):
-                    out[f, :, rg * 4 + j, t * 128 : (t + 1) * 128] = o[j]
+
+    def leave(g):
+        rows = pl.ds(pl.multiple_of(g * 8, 8), 8)
+        return pltpu.make_async_copy(held.at[:, rows], out.at[:, rows], sem.at[g])
+
+    @pl.loop(0, 8)
+    def _(g):
+        rows = pl.ds(pl.multiple_of(g * 8, 8), 8)
+        for f in range(3):
+            for t in range(2):
+                for rg in range(2):
+                    at = f * CELLS + rg * 128
+                    v = [
+                        ro[f, 4 * t + b, rows, rg * 128 : (rg + 1) * 128]
+                        + bo[4 * t + b, :, at : at + 128]
+                        for b in range(4)
+                    ]
+                    o = exchange_lanes(v, halves, evens)
+                    for j in range(4):
+                        held[f, rows, rg * 4 + j, t * 128 : (t + 1) * 128] = o[j]
+        leave(g).start()
+
+    for g in range(8):
+        leave(g).wait()
 
 
 def body(ensemble_state, obs_cell, obs_value, obs_prec):
@@ -637,16 +704,13 @@
             collective_id=0, has_side_effects=True, vmem_limit_bytes=40 << 20
         ),
         name="letkf_cycle",
-    )(ensemble_state, obs_cell, obs_value, obs_prec)
+    )(*(pltpu.with_memory_space_constraint(a, pltpu.HBM) for a in (ensemble_state, obs_cell, obs_value, obs_prec)))
     return pl.pallas_call(
         unpack,
-        grid=(8,),
         out_shape=jax.ShapeDtypeStruct((3, LOC, ROWS, LON), F32),
-        in_specs=[
-            pl.BlockSpec((3, NM, 8, CELLS), lambda g: (0, 0, g, 0)),
-            pl.BlockSpec((NM, 8, 768), lambda g: (0, 0, 0)),
-        ],
-        out_specs=pl.BlockSpec((3, 8, ROWS, LON), lambda g: (0, g, 0, 0)),
+        in_specs=[vmem, vmem],
+        out_specs=pl.BlockSpec(memory_space=pl.ANY),
+        scratch_shapes=[pltpu.VMEM((3, LOC, ROWS, LON), F32), dma((8,))],
         compiler_params=pltpu.CompilerParams(vmem_limit_bytes=16 << 20),
         name="unpack",
     )(received, biases)

time: 98.2 us -> 92 us (0.937)
  local copies, waits for them, and re-layouts: 4.12 us -> 0 us
  Pallas kernels: 93.9 us -> 91.2 us
    unnamed x8 -> x0, local copies, waits for them, and re-layouts: 4.12 us -> none
    pallas_call x1, Pallas kernels: 89.8 us -> 88.4 us  [body(): pl.pallas_call(kernel, out_shape=(jax.ShapeDtypeStruct((3, NM, LOC, CELLS...]
    pallas_call x1, Pallas kernels: 4.08 us -> 2.8 us  [body(): pl.pallas_call(unpack, out_shape=jax.ShapeDtypeStruct((3, LOC, ROWS, LON)...]
where the time goes in v2:
time: 92 us; the launch traced here: 91.4 us
  Pallas kernels  91.2 us (99%)
    pallas_call x1, Pallas kernels, body(): pl.pallas_call(kernel, out_shape=(jax.ShapeDtypeStruct((3, NM, LOC, CELLS...  88.4 us
    pallas_call x1, Pallas kernels, body(): pl.pallas_call(unpack, out_shape=jax.ShapeDtypeStruct((3, LOC, ROWS, LON)...  2.8 us

profile of v2, /device:TPU:0, one launch (start us, length us, event | category | flops | bytes accessed | tf_op | source)
XLA Modules:
  0.0 91.4 jit_solution(10618330512108224094)
XLA Ops:
  0.0 88.4 %letkf_cycle.1 = (f32[3,8,64,256]{3,2,1,0:T(8,128)S(1)}, f32[8,8,768]{2,1,0:T(8,128)S(1)}) custom-call(f32[3,64,8,256]{3,2,1,0:T(8,128)} %x_in.1, s32[16,8,256]{2,1,0:T(8,128)} %cell_in.1, f32[16,8,256]{2,1,0:T(8,128)} %val_in.1, f32[16,8,256]{2,1,0:T(8,128)} %prec_in.1), custom_call_target="tpu_custom_call" | custom-call | tf_op jit(solution)/shard_map/letkf_cycle/pallas_call | solution.py:654
  88.4 2.8 %unpack.1 = f32[3,64,8,256]{3,2,1,0:T(8,128)} custom-call(f32[3,8,64,256]{3,2,1,0:T(8,128)S(1)} %get-tuple-element.7.ro, f32[8,8,768]{2,1,0:T(8,128)S(1)} %get-tuple-element.8.bo), custom_call_target="tpu_custom_call" | custom-call | tf_op jit(solution)/shard_map/unpack/pallas_call | solution.py:708

commit v3 on v2

--- a/solution.py
+++ b/solution.py
@@ -60,9 +60,9 @@
 
 def kernel(
     x_in, cell_in, val_in, prec_in, ro, bo,
-    xn, cell, val, prec, xs, ht, hb, pk, rh, xf, sh, sl, s2h, s2l, g0, gs, gr, ds_, dr, co,
+    xn, cell, val, prec, xs, ht, hb, rl, pk, rh, xf, sh, sl, s2h, s2l, g0, gs, gr, ds_, dr, co,
     yh, yl, zh, zl, mh, ml, bh, bl, qh, ql, gh, gl, mf, rf, xh, xl, ao, bs,
-    in_sem, h_send, h_recv, o_send, o_recv, f_send, f_recv, g_send, g_recv, a_send, a_recv,
+    in_sem, h_send, h_recv, d_send, d_recv, r_send, o_send, o_recv, f_send, f_recv, g_send, g_recv, a_send, a_recv,
 ):
     me = lax.axis_index("member")
     lat = lax.axis_index("lat")
@@ -92,19 +92,17 @@
         pl.semaphore_signal(barrier, inc=1, device_id={"member": peer(k)}, device_id_type=MESH)
     for there in (north, south):
         pl.semaphore_signal(barrier, inc=1, device_id={"lat": there}, device_id_type=MESH)
-
-    with jax.named_scope("load"):
-
-        @pl.loop(0, 8)
-        def _(g):
-            state_in(g).wait()
-            rows = pl.ds(pl.multiple_of(g * 8, 8), 8)
-            for f in range(3):
-                for r in range(ROWS):
-                    xs[f, r, rows, :] = xn[f, rows, r, :]
-
-    with jax.named_scope("barrier"):
-        pl.semaphore_wait(barrier, NM + 1)
+    across = lax.rem(lat + NL // 2, NL)
+    mirrored = jnp.where(lat < NL // 2, NL // 2 - 1 - lat, 3 * NL // 2 - 1 - lat)
+    at_edge = (lat == 0) | (lat == NL - 1)
+    at_middle = (lat == NL // 2 - 1) | (lat == NL // 2)
+    at_corner = at_edge | at_middle
+
+    @pl.when(at_corner)
+    def _():
+        for there in (across, mirrored):
+            pl.semaphore_signal(barrier, inc=1, device_id={"lat": there}, device_id_type=MESH)
+
 
     def halo(side, g):
         rows = pl.ds(pl.multiple_of(g * 8, 8), 8)
@@ -117,15 +115,60 @@
 
     has_north, has_south = lat > 0, lat < NL - 1
 
-    @pl.when(has_north)
-    def _():
-        for g in range(8):
-            halo(0, g).start()
-
-    @pl.when(has_south)
-    def _():
-        for g in range(8):
-            halo(1, g).start()
+    def detour(side, g):
+        rows = pl.ds(pl.multiple_of(g * 8, 8), 8)
+        src = xs.at[:, 0:4, rows, :] if side == 0 else xs.at[:, 4:8, rows, :]
+        return pltpu.make_async_remote_copy(
+            src_ref=src, dst_ref=rl.at[:, :, rows, :], send_sem=d_send.at[g], recv_sem=d_recv.at[g],
+            device_id={"lat": across}, device_id_type=MESH,
+        )
+
+    def relay(side, g):
+        rows = pl.ds(pl.multiple_of(g * 8, 8), 8)
+        dst = (hb if side == 0 else ht).at[:, :, rows, :]
+        return pltpu.make_async_remote_copy(
+            src_ref=rl.at[:, :, rows, :], dst_ref=dst, send_sem=r_send.at[g], recv_sem=h_recv.at[side, g],
+            device_id={"lat": mirrored}, device_id_type=MESH,
+        )
+
+
+    with jax.named_scope("barrier"):
+
+        @pl.when(at_corner)
+        def _():
+            pl.semaphore_wait(barrier, NM + 3)
+
+        @pl.when(jnp.logical_not(at_corner))
+        def _():
+            pl.semaphore_wait(barrier, NM + 1)
+
+    with jax.named_scope("load"):
+
+        @pl.loop(0, 8)
+        def _(g):
+            state_in(g).wait()
+            rows = pl.ds(pl.multiple_of(g * 8, 8), 8)
+            for f in range(3):
+                for r in range(ROWS):
+                    xs[f, r, rows, :] = xn[f, rows, r, :]
+
+            by_relay = lax.rem(g, 2) == 1
+
+            @pl.when(has_north & jnp.logical_not((lat == NL // 2) & by_relay))
+            def _():
+                halo(0, g).start()
+
+            @pl.when(has_south & jnp.logical_not((lat == NL // 2 - 1) & by_relay))
+            def _():
+                halo(1, g).start()
+
+            @pl.when((lat == NL // 2) & by_relay)
+            def _():
+                detour(0, g).start()
+
+            @pl.when((lat == NL // 2 - 1) & by_relay)
+            def _():
+                detour(1, g).start()
 
     @pl.when(lat == 0)
     def _():
@@ -221,6 +264,18 @@
 
     @pl.loop(0, 8)
     def _(g):
+
+        @pl.when(at_edge & (lax.rem(g, 2) == 1))
+        def _():
+            detour(0, g).wait_recv()
+
+            @pl.when(lat == 0)
+            def _():
+                relay(0, g).start()
+
+            @pl.when(lat > 0)
+            def _():
+                relay(1, g).start()
 
         @pl.when(has_south)
         def _():
@@ -363,23 +418,47 @@
 
         return t_root * (co[b, 1:2, :] - y_bar * co[b, 0:1, :])
 
-    def products(h, l, i, j):
-        ri, rj = slice(i * 256, (i + 1) * 256), slice(j * 256, (j + 1) * 256)
-        acc = dot(h[ri, :], h[rj, :], NT) + dot(h[ri, :], l[rj, :], NT)
-        return acc + dot(l[ri, :], h[rj, :], NT)
+    def products(h, l):
+        left, right = slice(0, 256), slice(256, 512)
+        first = dot(h[left, :], h[left, :], NT) + dot(h[left, :], l[left, :], NT)
+        first = first + dot(l[left, :], h[left, :], NT)
+        both = dot(h[...], h[right, :], NT) + dot(h[...], l[right, :], NT)
+        both = both + dot(l[...], h[right, :], NT)
+        return [first, both[left], both[right]]
 
     for b in range(2):
         member_mean(b)
     drives = []
+    def west(a):
+        push = [weigh(a, b, sh, sl, b * CELLS) for b in range(2)]
+        for n, v in enumerate(products(sh, sl)):
+            if a < 2:
+                gs[a, n] = v
+            else:
+                g0[n] = v
+        return row_times(jnp.concatenate(push, axis=1), sh[...], sl[...], NT)
+
+    def east(a):
+        push = weigh(a, 2, s2h, s2l, 0)
+        for n, v in enumerate(products(s2h, s2l)):
+            if a < 2:
+                gs[a, n] = gs[a, n] + v
+            else:
+                g0[n] = g0[n] + v
+
+        def send():
+            for n in range(3):
+                for c in gram_copies(a, n):
+                    c.start()
+
+        if a < 2:
+            towards(a, send)
+        return row_times(push, s2h[...], s2l[...], NT)
+
+    drives = [None] * 3
     with jax.named_scope("gram01"):
-        for a in range(3):
-            push = [weigh(a, b, sh, sl, b * CELLS) for b in range(2)]
-            drives.append(row_times(jnp.concatenate(push, axis=1), sh[...], sl[...], NT))
-            for n, (i, j) in enumerate(BLOCKS):
-                if a < 2:
-                    gs[a, n] = products(sh, sl, i, j)
-                else:
-                    g0[n] = products(sh, sl, i, j)
+        for a in range(2):
+            drives[a] = west(a)
 
     with jax.named_scope("obs2"):
 
@@ -390,26 +469,14 @@
 
     member_mean(2)
     with jax.named_scope("gram2"):
-        for a in range(3):
-            push = weigh(a, 2, s2h, s2l, 0)
-            for n, (i, j) in enumerate(BLOCKS):
-                if a < 2:
-                    gs[a, n] = gs[a, n] + products(s2h, s2l, i, j)
-
-                    def send(a=a, n=n):
-                        for c in gram_copies(a, n):
-                            c.start()
-
-                    towards(a, send)
-                else:
-                    g0[n] = g0[n] + products(s2h, s2l, i, j)
-            drives[a] = drives[a] + row_times(push, s2h[...], s2l[...], NT)
-            if a < 2:
-                ds_[a] = jnp.broadcast_to(drives[a], (8, ENS))
-                towards(a, lambda a=a: drive_copy(a).start())
-            if a == 1:
-                for k in far_first:
-                    field_copy(k, True).start()
+        for a in range(2):
+            drives[a] = drives[a] + east(a)
+            ds_[a] = jnp.broadcast_to(drives[a], (8, ENS))
+            towards(a, lambda a=a: drive_copy(a).start())
+
+    with jax.named_scope("gramown"):
+        drives[2] = west(2)
+        drives[2] = drives[2] + east(2)
 
     with jax.named_scope("gwait"):
         for a in range(2):
@@ -421,6 +488,8 @@
                 drive_copy(a).wait_recv()
 
             towards(a, arrive)
+    for k in far_first:
+        field_copy(k, True).start()
     drive = drives[2] + dr[0, 0:1, :] + dr[1, 0:1, :]
 
     squares = jnp.zeros((8, 128), F32)
@@ -583,13 +652,23 @@
     @pl.loop(0, 8)
     def _(g):
 
-        @pl.when(has_north)
+        by_relay = lax.rem(g, 2) == 1
+
+        @pl.when(has_north & jnp.logical_not((lat == NL // 2) & by_relay))
         def _():
             halo(0, g).wait_send()
 
-        @pl.when(has_south)
+        @pl.when(has_south & jnp.logical_not((lat == NL // 2 - 1) & by_relay))
         def _():
             halo(1, g).wait_send()
+
+        @pl.when(at_middle & by_relay)
+        def _():
+            detour(0, g).wait_send()
+
+        @pl.when(at_edge & by_relay)
+        def _():
+            relay(0, g).wait_send()
 
         for k in range(1, NM):
             obs_copy(g, k, True).wait_send()
@@ -665,6 +744,7 @@
             pltpu.VMEM((8, 256), F32),
             pltpu.VMEM((8, 256), F32),
             pltpu.VMEM((3, ROWS, LOC, LON), F32),
+            pltpu.VMEM((3, 4, LOC, LON), F32),
             pltpu.VMEM((3, 4, LOC, LON), F32),
             pltpu.VMEM((3, 4, LOC, LON), F32),
             pltpu.VMEM((3, 10, LOC, CELLS), F32),
@@ -691,6 +771,9 @@
             dma((11,)),
             dma((2, 8)),
             dma((2, 8)),
+            dma((8,)),
+            dma((8,)),
+            dma((8,)),
             dma((9, 8)),
             dma((9, 8)),
             dma((8,)),

time: 92 us -> 91 us (0.989)
  Pallas kernels: 91.2 us -> 89.8 us
    pallas_call x1, Pallas kernels: 88.4 us -> 87 us  [body(): pl.pallas_call(kernel, out_shape=(jax.ShapeDtypeStruct((3, NM, LOC, CELLS...]
where the time goes in v3:
time: 91 us; the launch traced here: 90 us
  Pallas kernels  89.8 us (99%)
    pallas_call x1, Pallas kernels, body(): pl.pallas_call(kernel, out_shape=(jax.ShapeDtypeStruct((3, NM, LOC, CELLS...  87 us
    pallas_call x1, Pallas kernels, body(): pl.pallas_call(unpack, out_shape=jax.ShapeDtypeStruct((3, LOC, ROWS, LON)...  2.8 us

profile of v3, /device:TPU:0, one launch (start us, length us, event | category | flops | bytes accessed | tf_op | source)
XLA Modules:
  0.0 90.0 jit_solution(11599639373954236625)
XLA Ops:
  0.0 87.0 %letkf_cycle.1 = (f32[3,8,64,256]{3,2,1,0:T(8,128)S(1)}, f32[8,8,768]{2,1,0:T(8,128)S(1)}) custom-call(f32[3,64,8,256]{3,2,1,0:T(8,128)} %x_in.1, s32[16,8,256]{2,1,0:T(8,128)} %cell_in.1, f32[16,8,256]{2,1,0:T(8,128)} %val_in.1, f32[16,8,256]{2,1,0:T(8,128)} %prec_in.1), custom_call_target="tpu_custom_call" | custom-call | tf_op jit(solution)/shard_map/letkf_cycle/pallas_call | solution.py:733
  87.0 2.8 %unpack.1 = f32[3,64,8,256]{3,2,1,0:T(8,128)} custom-call(f32[3,8,64,256]{3,2,1,0:T(8,128)S(1)} %get-tuple-element.7.ro, f32[8,8,768]{2,1,0:T(8,128)S(1)} %get-tuple-element.8.bo), custom_call_target="tpu_custom_call" | custom-call | tf_op jit(solution)/shard_map/unpack/pallas_call | solution.py:791

commit v4 on v3

--- a/solution.py
+++ b/solution.py
@@ -440,19 +440,26 @@
 
     def east(a):
         push = weigh(a, 2, s2h, s2l, 0)
-        for n, v in enumerate(products(s2h, s2l)):
-            if a < 2:
-                gs[a, n] = gs[a, n] + v
-            else:
+        left, right = slice(0, 256), slice(256, 512)
+
+        def keep(n, v):
+            if a == 2:
                 g0[n] = g0[n] + v
-
-        def send():
-            for n in range(3):
+                return
+            gs[a, n] = gs[a, n] + v
+
+            def send():
                 for c in gram_copies(a, n):
                     c.start()
 
-        if a < 2:
             towards(a, send)
+
+        first = dot(s2h[left, :], s2h[left, :], NT) + dot(s2h[left, :], s2l[left, :], NT)
+        keep(0, first + dot(s2l[left, :], s2h[left, :], NT))
+        both = dot(s2h[...], s2h[right, :], NT) + dot(s2h[...], s2l[right, :], NT)
+        both = both + dot(s2l[...], s2h[right, :], NT)
+        keep(1, both[left])
+        keep(2, both[right])
         return row_times(push, s2h[...], s2l[...], NT)
 
     drives = [None] * 3
@@ -478,6 +485,22 @@
         drives[2] = west(2)
         drives[2] = drives[2] + east(2)
 
+    def take_states(f):
+        ref = rh.at[1] if f == 0 else xf.at[f - 1]
+        if f == 0:
+            bar = co[1, 2:3, :]
+        else:
+            bar = jnp.sum(ref[...], axis=0, keepdims=True) * (1.0 / ENS)
+        bs[0:1, f * CELLS : (f + 1) * CELLS] = bar
+
+        @pl.loop(0, ENS // 64)
+        def _(n):
+            r = pl.ds(pl.multiple_of(n * 64, 64), 64)
+            x_h, x_l = split(ref[r, :] - bar)
+            xh[r, f * CELLS : (f + 1) * CELLS] = x_h
+            xl[r, f * CELLS : (f + 1) * CELLS] = x_l
+
+    take_states(0)
     with jax.named_scope("gwait"):
         for a in range(2):
 
@@ -551,21 +574,6 @@
         for (i, j), v in zip(BLOCKS, new):
             put(to_h, to_l, i, j, v)
 
-    def take_states(f):
-        ref = rh.at[1] if f == 0 else xf.at[f - 1]
-        if f == 0:
-            bar = co[1, 2:3, :]
-        else:
-            bar = jnp.sum(ref[...], axis=0, keepdims=True) * (1.0 / ENS)
-        bs[0:1, f * CELLS : (f + 1) * CELLS] = bar
-
-        @pl.loop(0, ENS // 64)
-        def _(n):
-            r = pl.ds(pl.multiple_of(n * 64, 64), 64)
-            x_h, x_l = split(ref[r, :] - bar)
-            xh[r, f * CELLS : (f + 1) * CELLS] = x_h
-            xl[r, f * CELLS : (f + 1) * CELLS] = x_l
-
     for n, (i, j) in enumerate(BLOCKS):
         scaled = g0[n] * inv_fro
         mf[span(i), span(j)] = scaled
@@ -594,7 +602,7 @@
         for k in range(1, NM):
             field_copy(k, False).wait_recv()
     with jax.named_scope("states"):
-        for f in range(3):
+        for f in range(1, 3):
             take_states(f)
 
     with jax.named_scope("ns5"):
@@ -612,10 +620,11 @@
             device_id={"member": d}, device_id_type=MESH,
         )
 
-    def analysed(d):
-        r = pl.ds(pl.multiple_of(d * LOC, LOC), LOC)
-        both = dot(jnp.concatenate([zh[r, :], zl[r, :]], axis=0), xh[...])
-        acc = both[0:LOC] + both[LOC : 2 * LOC] + dot(zh[r, :], xl[...])
+    def analysed(d, e):
+        r = [pl.ds(pl.multiple_of(i * LOC, LOC), LOC) for i in (d, e)]
+        high = jnp.concatenate([zh[i, :] for i in r], axis=0)
+        both = dot(jnp.concatenate([high] + [zl[i, :] for i in r], axis=0), xh[...])
+        acc = both[0 : 2 * LOC] + both[2 * LOC : 4 * LOC] + dot(high, xl[...])
         return acc * scale
 
     def bias_copy(k, mine):
@@ -628,16 +637,17 @@
         )
 
 
-    for k in far_first:
-        d = peer(k)
-        r = pl.ds(pl.multiple_of(d * LOC, LOC), LOC)
-        res = analysed(d)
-        for f in range(3):
-            ao[f, r, :] = res[:, f * CELLS : (f + 1) * CELLS]
-        analysis_copy(k, True).start()
-    res = analysed(me)
-    for f in range(3):
-        ro[f, me, :, :] = res[:, f * CELLS : (f + 1) * CELLS]
+    for pair in ((4, 2), (6, 3), (5, 1), (7, 0)):
+        res = analysed(*(peer(k) for k in pair))
+        for n, k in enumerate(pair):
+            for f in range(3):
+                part = res[n * LOC : (n + 1) * LOC, f * CELLS : (f + 1) * CELLS]
+                if k:
+                    ao[f, pl.ds(pl.multiple_of(peer(k) * LOC, LOC), LOC), :] = part
+                else:
+                    ro[f, me, :, :] = part
+            if k:
+                analysis_copy(k, True).start()
     mean_weight = row_times(row_times(drive, zh[...], zl[...]), zh[...], zl[...]) * inv_fro
     bias = bs[0:1, :] + row_times(mean_weight, xh[...], xl[...])
     bs[...] = jnp.broadcast_to(bias, (8, 768))

time: 91 us -> 90.3 us (level)
  Pallas kernels: 89.8 us -> 88.8 us
    pallas_call x1, Pallas kernels: 87 us -> 86 us  [body(): pl.pallas_call(kernel, out_shape=(jax.ShapeDtypeStruct((3, NM, LOC, CELLS...]
where the time goes in v4:
time: 90.3 us; the launch traced here: 89 us
  Pallas kernels  88.8 us (98%)
    pallas_call x1, Pallas kernels, body(): pl.pallas_call(kernel, out_shape=(jax.ShapeDtypeStruct((3, NM, LOC, CELLS...  86 us
    pallas_call x1, Pallas kernels, body(): pl.pallas_call(unpack, out_shape=jax.ShapeDtypeStruct((3, LOC, ROWS, LON)...  2.8 us

profile of v4, /device:TPU:0, one launch (start us, length us, event | category | flops | bytes accessed | tf_op | source)
XLA Modules:
  0.0 89.0 jit_solution(9733288292033784987)
XLA Ops:
  0.0 86.0 %letkf_cycle.1 = (f32[3,8,64,256]{3,2,1,0:T(8,128)S(1)}, f32[8,8,768]{2,1,0:T(8,128)S(1)}) custom-call(f32[3,64,8,256]{3,2,1,0:T(8,128)} %x_in.1, s32[16,8,256]{2,1,0:T(8,128)} %cell_in.1, f32[16,8,256]{2,1,0:T(8,128)} %val_in.1, f32[16,8,256]{2,1,0:T(8,128)} %prec_in.1), custom_call_target="tpu_custom_call" | custom-call | tf_op jit(solution)/shard_map/letkf_cycle/pallas_call | solution.py:743
  86.0 2.8 %unpack.1 = f32[3,64,8,256]{3,2,1,0:T(8,128)} custom-call(f32[3,8,64,256]{3,2,1,0:T(8,128)S(1)} %get-tuple-element.7.ro, f32[8,8,768]{2,1,0:T(8,128)S(1)} %get-tuple-element.8.bo), custom_call_target="tpu_custom_call" | custom-call | tf_op jit(solution)/shard_map/unpack/pallas_call | solution.py:801

commit v5 on v4

--- a/solution.py
+++ b/solution.py
@@ -61,7 +61,7 @@
 def kernel(
     x_in, cell_in, val_in, prec_in, ro, bo,
     xn, cell, val, prec, xs, ht, hb, rl, pk, rh, xf, sh, sl, s2h, s2l, g0, gs, gr, ds_, dr, co,
-    yh, yl, zh, zl, mh, ml, bh, bl, qh, ql, gh, gl, mf, rf, xh, xl, ao, bs,
+    yh, yl, zh, zl, mh, ml, bh, bl, qh, ql, gh, gl, mf, rf, xh, xl, ao, bs, bd,
     in_sem, h_send, h_recv, d_send, d_recv, r_send, o_send, o_recv, f_send, f_recv, g_send, g_recv, a_send, a_recv,
 ):
     me = lax.axis_index("member")
@@ -631,7 +631,7 @@
         d = peer(k)
         owner = me if mine else source(k)
         return pltpu.make_async_remote_copy(
-            src_ref=bs, dst_ref=bo.at[owner],
+            src_ref=bd, dst_ref=bo.at[owner],
             send_sem=a_send.at[1, k], recv_sem=a_recv.at[1, k],
             device_id={"member": d}, device_id_type=MESH,
         )
@@ -650,8 +650,10 @@
                 analysis_copy(k, True).start()
     mean_weight = row_times(row_times(drive, zh[...], zl[...]), zh[...], zl[...]) * inv_fro
     bias = bs[0:1, :] + row_times(mean_weight, xh[...], xl[...])
-    bs[...] = jnp.broadcast_to(bias, (8, 768))
-    bo[me] = jnp.broadcast_to(bias, (8, 768))
+    lines = [bias[:, i * 128 : (i + 1) * 128] for i in range(6)]
+    packed = jnp.concatenate(lines + [jnp.zeros((2, 128), F32)], axis=0)
+    bd[...] = packed
+    bo[me] = packed
     for k in far_first:
         bias_copy(k, True).start()
     with jax.named_scope("out"):
@@ -719,10 +721,10 @@
         for f in range(3):
             for t in range(2):
                 for rg in range(2):
-                    at = f * CELLS + rg * 128
+                    at = 2 * f + rg
                     v = [
                         ro[f, 4 * t + b, rows, rg * 128 : (rg + 1) * 128]
-                        + bo[4 * t + b, :, at : at + 128]
+                        + bo[4 * t + b, at : at + 1, :]
                         for b in range(4)
                     ]
                     o = exchange_lanes(v, halves, evens)
@@ -744,7 +746,7 @@
         kernel,
         out_shape=(
             jax.ShapeDtypeStruct((3, NM, LOC, CELLS), F32),
-            jax.ShapeDtypeStruct((NM, 8, 768), F32),
+            jax.ShapeDtypeStruct((NM, 8, 128), F32),
         ),
         in_specs=[anywhere] * 4,
         out_specs=(vmem, vmem),
@@ -778,6 +780,7 @@
             pltpu.VMEM((ENS, 768), BF16),
             pltpu.VMEM((3, ENS, CELLS), F32),
             pltpu.VMEM((8, 768), F32),
+            pltpu.VMEM((8, 128), F32),
             dma((11,)),
             dma((2, 8)),
             dma((2, 8)),

time: 90.3 us -> 88.5 us (0.980)
  Pallas kernels: 88.8 us -> 86.9 us
    pallas_call x1, Pallas kernels: 86 us -> 84.1 us  [body(): pl.pallas_call(kernel, out_shape=(jax.ShapeDtypeStruct((3, NM, LOC, CELLS...]
where the time goes in v5:
time: 88.5 us; the launch traced here: 87.1 us
  Pallas kernels  86.9 us (98%)
    pallas_call x1, Pallas kernels, body(): pl.pallas_call(kernel, out_shape=(jax.ShapeDtypeStruct((3, NM, LOC, CELLS...  84.1 us
    pallas_call x1, Pallas kernels, body(): pl.pallas_call(unpack, out_shape=jax.ShapeDtypeStruct((3, LOC, ROWS, LON)...  2.81 us

profile of v5, /device:TPU:0, one launch (start us, length us, event | category | flops | bytes accessed | tf_op | source)
XLA Modules:
  0.0 87.1 jit_solution(14479961396869614871)
XLA Ops:
  0.0 84.1 %letkf_cycle.1 = (f32[3,8,64,256]{3,2,1,0:T(8,128)S(1)}, f32[8,8,128]{2,1,0:T(8,128)S(1)}) custom-call(f32[3,64,8,256]{3,2,1,0:T(8,128)} %x_in.1, s32[16,8,256]{2,1,0:T(8,128)} %cell_in.1, f32[16,8,256]{2,1,0:T(8,128)} %val_in.1, f32[16,8,256]{2,1,0:T(8,128)} %prec_in.1), custom_call_target="tpu_custom_call" | custom-call | tf_op jit(solution)/shard_map/letkf_cycle/pallas_call | solution.py:745
  84.1 2.8 %unpack.1 = f32[3,64,8,256]{3,2,1,0:T(8,128)} custom-call(f32[3,8,64,256]{3,2,1,0:T(8,128)S(1)} %get-tuple-element.7.ro, f32[8,8,128]{2,1,0:T(8,128)S(1)} %get-tuple-element.8.bo), custom_call_target="tpu_custom_call" | custom-call | tf_op jit(solution)/shard_map/unpack/pallas_call | solution.py:804
